TPU v7x, 8 devices: a whole 2x2x1 slice. The times are simulated.
8 devices in a mesh: dp: 2 (over z, y), ep: 4 (over x, core).
Axes of the slice: x: 2, y: 2, z: 1, core: 2. Of those that a mesh axis runs over, the one named last changes fastest.
Arguments:
- tokens: bfloat16 [8192, 768], P(('dp', 'ep')), parts along dimension 0
- choice_idx: int32 [64, 128], P(('dp', 'ep')), parts along dimension 0
- gate_weight: float32 [64, 128], P(('dp', 'ep')), parts along dimension 0
- w_in: bfloat16 [32, 768, 3072], P('ep')
- w_out: bfloat16 [32, 3072, 768], P('ep')
Outputs:
- output: bfloat16 [8192, 768], P(('dp', 'ep')), parts along dimension 0
There are 2 independent parts. A program takes and returns all parts, laid end to end along the dimension named above; an argument that names none is the same for every part.
All inputs are finite; a program needn't handle non-finite values.
Results may differ from a plain program's by a relative error of at most 0.001.
Values are sent between devices in bfloat16 or wider.
A program may use at most 1 GiB of HBM per device.

v0:
```python
import functools

import jax
import jax.numpy as jnp
from jax import lax
from jax.experimental import pallas as pl
from jax.experimental.pallas import tpu as pltpu
from jax.sharding import PartitionSpec as P

F32, BF16, I32 = jnp.float32, jnp.bfloat16, jnp.int32
W_SLOTS = 3
LANES = 128
FAR = 1 << 20
LENGTHS = ((1, 2), (2, 4), (3, 6), (5, 8), (8, 8))


def remote(src, dst, ss, rs, **dev):
    return pltpu.make_async_remote_copy(src_ref=src, dst_ref=dst, send_sem=ss, recv_sem=rs,
                                        device_id=dev, device_id_type=pl.DeviceIdType.MESH)


def signal(sem, **dev):
    pl.semaphore_signal(sem, inc=1, device_id=dev, device_id_type=pl.DeviceIdType.MESH)


def spread(col, width, lane):
    return jnp.concatenate(
        [jnp.where(col == lane + LANES * j, 1.0, 0.0).astype(BF16) for j in range(width // LANES)], axis=1)


def column(row, cap):
    return jnp.broadcast_to(row, (LANES, cap)).T


def table(pos, his, los):
    n = len(pos)
    sub_b = lax.broadcasted_iota(I32, (n, LANES), 0)
    sub_l = lax.broadcasted_iota(I32, (LANES, LANES), 0)
    blocks, his_b, los_b, lanes = [], [], [], []
    for p, hi, lo in zip(pos, his, los):
        b = jnp.where(jnp.broadcast_to(p >> 7, sub_b.shape) == sub_b, 1.0, 0.0)
        blocks.append(b.astype(BF16))
        his_b.append((b * hi.astype(F32)).astype(BF16))
        los_b.append((b * lo.astype(F32)).astype(BF16))
        lanes.append(jnp.where(jnp.broadcast_to(p & (LANES - 1), sub_l.shape) == sub_l, 1.0, 0.0).astype(BF16))
    left = jnp.concatenate([jnp.concatenate(x, axis=1) for x in (blocks, his_b, los_b)], axis=0)
    out = lax.dot_general(left, jnp.concatenate(lanes, axis=1), (((1,), (1,)), ((), ())), preferred_element_type=F32)
    ids = (out[n:2 * n] * LANES + out[2 * n:3 * n]).astype(I32)
    return jnp.where(out[0:n] > 0.5, ids, -FAR)


def below(shape, key):
    r, c = (key(lax.broadcasted_iota(I32, shape, a)) for a in (0, 1))
    return jnp.where(c < r, 1.0, 0.0).astype(BF16)


def plan_kernel(n_dp, n_ep, sizes, tok, idx, chip_tok, xown, meta, bucket, idx_g, pick_s, loc_sem, idx_ss, idx_rs, tok_ss, tok_rs):
    n_tok = tok.shape[0]
    n_exp, cap = idx.shape
    dp, ep = lax.axis_index("dp"), lax.axis_index("ep")
    me = dp * n_ep + ep
    n_dev = n_dp * n_ep
    core = lax.rem(ep, 2)
    own_rows = chip_tok.at[pl.ds(pl.multiple_of(core * n_tok, n_tok), n_tok)]
    own_idx = pltpu.make_async_copy(idx, idx_g.at[me], loc_sem.at[0])
    own_tok = pltpu.make_async_copy(tok, own_rows, loc_sem.at[1])
    own_idx.start()
    own_tok.start()
    barrier = pltpu.get_barrier_semaphore()
    offsets = [(a, b) for a in range(n_dp - 1, -1, -1) for b in range(n_ep - 1, -1, -1) if a or b]
    others = [(lax.rem(dp + a, n_dp), lax.rem(ep + b, n_ep)) for a, b in offsets]
    n_far = (n_dp - 1) * n_ep
    for d, e in others:
        signal(barrier, dp=d, ep=e)
    own_idx.wait()
    pl.semaphore_wait(barrier, n_dev - 1)
    for k, (d, e) in enumerate(others):
        remote(idx_g.at[me], idx_g.at[me], idx_ss, idx_rs.at[0 if k < n_far else 1], dp=d, ep=e).start()

    def blocks(n, k):
        r = idx_g.at[0:n]
        return remote(r, r, idx_ss, idx_rs.at[k], dp=dp, ep=ep + 1 - 2 * core)

    own_tok.wait()
    tok_out = remote(own_rows, own_rows, tok_ss, tok_rs, dp=dp, ep=ep + 1 - 2 * core)
    tok_out.start()
    lane = lax.broadcasted_iota(I32, (cap, LANES), 1)

    @pl.loop(0, n_exp // 2)
    def _(g):
        hot = jnp.concatenate(
            [spread(column(idx_g[me, pl.ds(2 * g + k, 1), :] - ep * n_tok, cap), n_tok, lane) for k in range(2)], axis=0)
        xown[pl.ds(pl.multiple_of(2 * g * cap, 2 * cap), 2 * cap), :] = jnp.dot(
            hot, own_rows[...], preferred_element_type=F32).astype(BF16)

    rows = 2 * n_exp
    half = 2 * n_tok
    t_lanes = LANES // 2
    t_rows = half // t_lanes

    upper_t = jnp.where(lax.broadcasted_iota(I32, (t_lanes, t_lanes), 0) < lax.broadcasted_iota(I32, (t_lanes, t_lanes), 1),
                        1.0, 0.0).astype(BF16)
    ones_t = jnp.ones((t_lanes, t_lanes), BF16)
    lower = below((n_exp * t_rows, n_exp * t_rows), lambda x: x)
    sub_hi = lax.broadcasted_iota(I32, (t_rows, cap), 0)
    sub_lo = lax.broadcasted_iota(I32, (t_lanes, cap), 0)

    def presence(d, h, e):
        his, los = [], []
        for c in range(2):
            at_chip = idx_g[d * n_ep + 2 * h + c, e:e + 1, :] - (1 - h) * half
            his.append(jnp.where(jnp.broadcast_to(at_chip >> 6, sub_hi.shape) == sub_hi, 1.0, 0.0).astype(BF16))
            los.append(jnp.where(jnp.broadcast_to(at_chip & (t_lanes - 1), sub_lo.shape) == sub_lo, 1.0, 0.0).astype(BF16))
        count = lax.dot_general(jnp.concatenate(his, axis=1), jnp.concatenate(los, axis=1),
                                (((1,), (1,)), ((), ())), preferred_element_type=F32)
        return jnp.minimum(count, 1.0)

    def crosses(d, h):
        ids = jnp.concatenate([idx_g[d * n_ep + 2 * h], idx_g[d * n_ep + 2 * h + 1]], axis=0)
        return ids, (ids >= half) if h == 0 else (ids < half)

    with jax.named_scope("A_near"):
        blocks(n_ep - 1, 1).wait_recv()

    distinct = most = None
    lists = []
    for h in range(2):
        seen = jnp.zeros((t_rows, t_lanes), F32)
        fresh = []
        for e in range(n_exp):
            here = presence(dp, h, e)
            fresh.append(here * (1.0 - seen))
            seen = jnp.maximum(seen, here)
        lists.append((seen, fresh))
        n = jnp.sum(seen)
        distinct = n if distinct is None else jnp.maximum(distinct, n)
        ids, need = crosses(dp, h)
        meta[0, h * rows:(h + 1) * rows, :] = ids
        n = jnp.sum(jnp.where(need, 1.0, 0.0))
        most = n if most is None else jnp.maximum(most, n)

    with jax.named_scope("A_far"):
        blocks(n_far, 0).wait_recv()

    for a in range(1, n_dp):
        d = lax.rem(dp + a, n_dp)
        for h in range(2):
            most = jnp.maximum(most, jnp.sum(jnp.where(crosses(d, h)[1], 1.0, 0.0)))
            seen = presence(d, h, 0)
            for e in range(1, n_exp):
                seen = jnp.maximum(seen, presence(d, h, e))
            distinct = jnp.maximum(distinct, jnp.sum(seen))
    pick = jnp.int32(0)
    for k_out, k_back in sizes[:-1]:
        pick = pick + jnp.where((distinct > k_out) | (most > k_back), 1, 0).astype(I32)
    pick_s[0] = pick
    pick_out = pltpu.make_async_copy(pick_s, bucket, loc_sem.at[2])
    pick_out.start()

    for h, (seen, fresh) in enumerate(lists):
        new = jnp.concatenate(fresh, axis=0)
        new_b = new.astype(BF16)
        row_sum = jnp.dot(new_b, ones_t, preferred_element_type=F32).astype(BF16)
        pos = (jnp.dot(new_b, upper_t, preferred_element_type=F32) + jnp.dot(lower, row_sum, preferred_element_type=F32)) * new
        place = jnp.zeros((t_rows, t_lanes), F32)
        for e in range(n_exp):
            place = place + pos[e * t_rows:(e + 1) * t_rows, :]
        place = jnp.where(seen > 0.5, place.astype(I32), FAR)
        meta[1, h * rows:(h + 1) * rows, :] = jnp.concatenate([place[0:t_rows // 2], place[t_rows // 2:]], axis=1)

    blocks(n_dev - 1, 0).wait_send()
    with jax.named_scope("A_tok"):
        tok_out.wait()
    pick_out.wait()


def layer_kernel(k_out, k_rows, chip_tok, xown, meta_v, gate_v, w_in, w_out, out,
                 xsend, land, local, xbuf, chip_p, pland, rsend, rland, listtok, tokrow, back_at, hot_last, acc, sum_o, wi, wo,
                 w_sem, d_ss, d_rs, f_ss, f_rs, p_ss, p_rs, r_ss, r_rs, g_ss, g_rs):
    n_tok, d_model = out.shape
    n_exp, d_ff = w_in.shape[0], w_in.shape[2]
    cap = gate_v.shape[1]
    slots = n_exp * cap
    rows = 2 * n_exp
    n_list = k_rows // cap
    assert n_list % 2 == 0
    nc = n_list // 2
    n_out = k_out // cap
    no = (n_out + 1) // 2
    ep = lax.axis_index("ep")
    chip, core = ep // 2, ep % 2
    mate = chip * 2 + (1 - core)
    opp = (1 - chip) * 2 + core

    def at(start, size):
        return pl.ds(start if isinstance(start, int) else pl.multiple_of(start, cap), size)

    def w_copies(e):
        slot = lax.rem(e, W_SLOTS)
        return (pltpu.make_async_copy(w_in.at[e], wi.at[slot], w_sem.at[0, slot]),
                pltpu.make_async_copy(w_out.at[e], wo.at[slot], w_sem.at[1, slot]))

    barrier = pltpu.get_barrier_semaphore()
    signal(barrier, ep=mate)
    signal(barrier, ep=opp)
    for e in range(W_SLOTS):
        for c in w_copies(e):
            c.start()

    def d_copy(m):
        return remote(xsend.at[at(m * cap, cap)], land.at[at((2 * m + core) * cap, cap)], d_ss, d_rs.at[m], ep=opp)

    def f_copy(m):
        r = at((2 * m + core) * cap, cap)
        return remote(land.at[r], land.at[r], f_ss, f_rs.at[m], ep=mate)

    def p_copy(e):
        return remote(chip_p.at[at(core * slots + e * cap, cap)], pland.at[at(e * cap, cap)], p_ss, p_rs.at[e], ep=mate)

    def r_copy(m):
        return remote(rsend.at[at(m * cap, cap)], rland.at[at((2 * m + core) * cap, cap)], r_ss, r_rs.at[m], ep=opp)

    def g_copy(m):
        r = at((2 * m + core) * cap, cap)
        return remote(rland.at[r], rland.at[r], g_ss, g_rs.at[m], ep=mate)

    def if_in(block, total, f):
        if total % 2:
            pl.when(block < total)(f)
        else:
            f()

    lane = lax.broadcasted_iota(I32, (cap, LANES), 1)
    sub = lax.broadcasted_iota(I32, (cap, LANES), 0)
    t_half = LANES // 2

    def tokens_of(lanes, i):
        return jnp.where(lanes < t_half, lanes, lanes + (n_tok - t_half)) + t_half * i

    their = (1 - chip) * rows
    mine = chip * rows

    def gather_block(m):
        t = jnp.zeros((cap, LANES), I32)
        for i in range(rows):
            pos = meta_v[1, pl.ds(their + i, 1), :]
            t = t + jnp.where(jnp.broadcast_to(pos, (cap, LANES)) == sub + (2 * m + core) * cap, tokens_of(lane, i), 0)
        at_chip = jnp.sum(t.astype(F32), axis=1, keepdims=True).astype(I32)
        return spread(jnp.broadcast_to(at_chip, (cap, LANES)), 2 * n_tok, lane)

    @pl.loop(0, no)
    def _(m):
        with jax.named_scope("send_group"):
            xsend[at(m * cap, cap), :] = jnp.dot(gather_block(m), chip_tok[...], preferred_element_type=F32).astype(BF16)

        @pl.when(m == 0)
        def _():
            pl.semaphore_wait(barrier, 2)

        pl.when(2 * m + core < n_out)(lambda: d_copy(m).start())

    mate_rows = at((1 - core) * n_tok, n_tok)

    @pl.loop(0, n_exp // 2)
    def _(g):
        with jax.named_scope("own_gather"):
            hot = jnp.concatenate(
                [spread(column(meta_v[0, pl.ds(mine + core * n_exp + 2 * g + k, 1), :] - mate * n_tok, cap), n_tok, lane)
                 for k in range(2)], axis=0)
            r = at(2 * g * cap, 2 * cap)
            xbuf[r, :] = xown[r, :] + jnp.dot(hot, chip_tok[mate_rows, :], preferred_element_type=F32).astype(BF16)

    @pl.loop(0, no)
    def _(b):
        local[at(b * 2 * cap, 2 * cap), :] = jnp.zeros((2 * cap, d_model), BF16)

    @pl.loop(0, n_exp)
    def _(b):
        chip_p[at(b * 2 * cap, 2 * cap), :] = jnp.zeros((2 * cap, d_model), BF16)

    def forward(m):
        def go():
            with jax.named_scope("forward"):
                d_copy(m).wait_recv()
                f_copy(m).start()

        if_in(2 * m + core, n_out, go)

    lane_row = lax.broadcasted_iota(I32, (1, LANES), 1)
    listtok[...] = table([meta_v[1, pl.ds(mine + i, 1), :] for i in range(rows)],
                         [tokens_of(lane_row, i) >> 7 for i in range(rows)],
                         [tokens_of(lane_row, i) & (LANES - 1) for i in range(rows)])
    before = below((rows, rows), lambda x: lax.rem(x, n_exp) * 2 + x // n_exp) - jnp.ones((rows, rows), BF16)
    upper = below((cap, cap), lambda x: -x)
    ones = jnp.ones((cap, cap), BF16)
    for h in range(2):
        ids = meta_v[0, h * rows:(h + 1) * rows, :]
        need = (ids >= 2 * n_tok) if h == 0 else (ids < 2 * n_tok)
        flag = jnp.where(need, 1.0, 0.0).astype(BF16)
        slot_sum = jnp.dot(flag, ones, preferred_element_type=F32).astype(BF16)
        place = jnp.dot(flag, upper, preferred_element_type=F32) + jnp.dot(before, slot_sum, preferred_element_type=F32)
        back_at[h * rows:(h + 1) * rows, :] = jnp.where(need, place.astype(I32) + k_rows, FAR)

    forward(0)

    back_pos = [back_at[pl.ds(their + i, 1), :] for i in range(rows)]
    back_ids = [meta_v[0, pl.ds(their + i, 1), :] for i in range(rows)]
    tokrow[...] = table(back_pos, [i >> 7 for i in back_ids], [i & (LANES - 1) for i in back_ids])
    f_tile = 1536
    n_f = d_ff // f_tile

    def m_of(e):
        return e - (n_exp - nc)

    def pack_return(e):
        with jax.named_scope("pwait"):
            p_copy(e).wait_recv()
        chip_p[at((1 - core) * slots + e * cap, cap), :] = pland[at(e * cap, cap), :]
        m = m_of(e)

        @pl.when(m >= 0)
        def _():
            parts = []
            for i in range(rows):
                pos = back_at[pl.ds(mine + i, 1), :]
                parts.append(jnp.where(jnp.broadcast_to(pos, (cap, LANES)) == sub + (2 * m + core) * cap, 1.0, 0.0).astype(BF16))
            hot = jnp.concatenate(parts, axis=1)
            rsend[at(m * cap, cap), :] = jnp.dot(hot, chip_p[...], preferred_element_type=F32).astype(BF16)
            r_copy(m).start()

    @pl.loop(0, n_exp)
    def _(e):
        slot = lax.rem(e, W_SLOTS)

        mine_e = at(e * cap, cap)

        def take_block():
            def go():
                with jax.named_scope("fwait"):
                    f_copy(e).wait_recv()

            if_in(2 * e + 1 - core, n_out, go)
            for k in range(2):
                @pl.when(2 * e + k < n_out)
                def _():
                    r = at((2 * e + k) * cap, cap)
                    local[r, :] = land[r, :]

        def fill():
            pl.when(e < no)(take_block)
            wanted = column(meta_v[0, pl.ds(mine + core * n_exp + e, 1), :], cap) - (1 - chip) * (2 * n_tok)
            hot = jnp.concatenate(
                [jnp.where(wanted == jnp.broadcast_to(listtok[j:j + 1, :], (cap, LANES)), 1.0, 0.0).astype(BF16)
                 for j in range(n_out)], axis=1)
            xbuf[mine_e, :] = xbuf[mine_e, :] + jnp.dot(hot, local[0:k_out, :], preferred_element_type=F32).astype(BF16)
            with jax.named_scope("wwait"):
                for c in w_copies(e):
                    c.wait()
            sum_o[...] = jnp.zeros((cap, d_model), F32)

        soon = (m_of(e - 1) == 0) | (m_of(e - 1) == 1)

        @pl.loop(0, 2)
        def _(half):
            @pl.when((e > 0) & ((half == 0) == soon))
            def _():
                pack_return(e - 1)

            pl.when(half == 0)(fill)

            @pl.when((half == 1) & (e + 1 < no) & (m_of(e) != 0) & (m_of(e) != 1))
            def _():
                forward(e + 1)

            x = xbuf[mine_e, :]
            o = None
            for f in range(n_f // 2):
                fs = at(half * (d_ff // 2) + f * f_tile, f_tile)
                pre = jnp.dot(x, wi[slot, :, fs], preferred_element_type=F32)
                h = jax.nn.gelu(pre, approximate=True).astype(BF16)
                part = jnp.dot(h, wo[slot, fs, :], preferred_element_type=F32)
                o = part if o is None else o + part
            sum_o[...] = sum_o[...] + o

        gcol = column(gate_v[pl.ds(e, 1), :], cap)
        chip_p[at(core * slots + e * cap, cap), :] = (
            jnp.concatenate([gcol] * (d_model // LANES), axis=1) * sum_o[...]).astype(BF16)
        p_copy(e).start()

        @pl.when((e + 1 < no) & ((m_of(e) == 0) | (m_of(e) == 1)))
        def _():
            forward(e + 1)

        @pl.when(e + W_SLOTS < n_exp)
        def _():
            for c in w_copies(e + W_SLOTS):
                c.start()

    n_blk = n_tok // (2 * cap)
    blk = 2 * cap
    sub_b = lax.broadcasted_iota(I32, (blk, LANES), 0) + ep * n_tok
    early = min(nc - 3, 10 - nc)

    def forward_back(m):
        with jax.named_scope("rwait"):
            r_copy(m).wait_recv()
            g_copy(m).start()

    def back_wait(m):
        with jax.named_scope("gwait"):
            g_copy(m).wait_recv()

    pl.loop(0, early)(forward_back)
    with jax.named_scope("pack_last"):
        pack_return(n_exp - 1)
    pl.loop(0, early)(back_wait)

    def owners(row, b):
        return jnp.where(jnp.broadcast_to(row, (blk, LANES)) == sub_b + b * blk, 1.0, 0.0).astype(BF16)

    @pl.loop(0, n_blk)
    def _(b):
        with jax.named_scope("early_back"):
            hot = jnp.concatenate([owners(tokrow[pl.ds(i, 1), :], b) for i in range(2 * early)], axis=1)
            own = chip_tok[at(core * n_tok + b * blk, blk), :].astype(F32)
            acc[at(b * blk, blk), :] = own + jnp.dot(hot, rland[0:early * 2 * cap, :], preferred_element_type=F32)

    @pl.loop(0, n_blk)
    def _(b):
        @pl.when(b == n_blk // 2)
        def _():
            forward_back(early)

        with jax.named_scope("own_scatter"):
            r = at(b * blk, blk)
            hot = jnp.concatenate([owners(meta_v[0, pl.ds(mine + i, 1), :], b) for i in range(rows)], axis=1)
            acc[r, :] = acc[r, :] + jnp.dot(hot, chip_p[...], preferred_element_type=F32)

    def combine(m):
        ids = [tokrow[pl.ds(2 * m + k, 1), :] for k in range(2)]
        back_wait(m)
        back = rland[at(2 * m * cap, 2 * cap), :]

        @pl.loop(0, n_blk)
        def _(b):
            r = at(b * blk, blk)
            hot = jnp.concatenate([owners(i, b) for i in ids], axis=1)
            acc[r, :] = acc[r, :] + jnp.dot(hot, back, preferred_element_type=F32)

    last = nc - 1

    @pl.loop(0, n_blk)
    def _(b):
        hot_last[at(b * blk, blk), :] = jnp.concatenate(
            [owners(tokrow[2 * last + k:2 * last + k + 1, :], b) for k in range(2)], axis=1)

    def sent(sem, buf, blocks):
        r = buf.at[0:blocks * cap]
        remote(r, r, sem, sem, ep=mate).wait_send()

    def sent_out(blocks):
        sent(d_ss, xsend, blocks)
        sent(f_ss, land, blocks)

    if n_out % 2:
        pl.when(core == 0)(lambda: sent_out(no))
        pl.when(core == 1)(lambda: sent_out(no - 1))
    else:
        sent_out(no)
    sent(p_ss, chip_p, n_exp)

    @pl.loop(early, nc - 2)
    def _(m):
        forward_back(m + 1)
        combine(m)

    combine(nc - 2)
    forward_back(last)
    sent(r_ss, rsend, nc)
    back_wait(last)
    with jax.named_scope("last_add"):
        back = rland[2 * last * cap:2 * nc * cap, :]
        for b in range(n_blk):
            r = at(b * blk, blk)
            out[r, :] = (acc[r, :] + jnp.dot(hot_last[r, :], back, preferred_element_type=F32)).astype(BF16)

    sent(g_ss, rland, nc)


def solution(mesh):
    n_dp, n_ep = mesh.shape["dp"], mesh.shape["ep"]
    row_spec = P(("dp", "ep"), None)
    expert_spec = P("ep", None, None)
    dma = pltpu.SemaphoreType.DMA
    any_spec = pl.BlockSpec(memory_space=pl.ANY)
    vmem_spec = pl.BlockSpec(memory_space=pltpu.VMEM)

    def local_layer(tok, idx, gate, w_in, w_out):
        n_tok, d_model = tok.shape
        n_exp, cap = idx.shape
        d_ff = w_in.shape[2]
        slots = n_exp * cap
        sizes = tuple((slots + i * cap, slots + j * cap) for i, j in LENGTHS)
        n_dev = n_dp * n_ep

        chip_tok, xown, meta, bucket = pl.pallas_call(
            functools.partial(plan_kernel, n_dp, n_ep, sizes),
            out_shape=(jax.ShapeDtypeStruct((2 * n_tok, d_model), BF16),
                       jax.ShapeDtypeStruct((slots, d_model), BF16),
                       jax.ShapeDtypeStruct((2, 4 * n_exp, cap), I32),
                       jax.ShapeDtypeStruct((1,), I32)),
            in_specs=[any_spec] * 2,
            out_specs=(vmem_spec, vmem_spec, vmem_spec, any_spec),
            scratch_shapes=[
                pltpu.VMEM((n_dev, n_exp, cap), I32),
                pltpu.SMEM((1,), I32),
                dma((3,)), dma, dma((2,)), dma, dma,
            ],
            compiler_params=pltpu.CompilerParams(
                collective_id=0, has_side_effects=True, vmem_limit_bytes=58 * 1024 * 1024),
        )(tok, idx)

        def branch(i):
            k_out, k_rows = sizes[i]
            no = (k_out // cap + 1) // 2
            nc = k_rows // (2 * cap)

            def run(chip_tok, xown, meta, gate, w_in, w_out):
                return pl.pallas_call(
                    functools.partial(layer_kernel, k_out, k_rows),
                    out_shape=jax.ShapeDtypeStruct((n_tok, d_model), BF16),
                    in_specs=[vmem_spec] * 4 + [any_spec] * 2,
                    out_specs=vmem_spec,
                    scratch_shapes=[
                        pltpu.VMEM((no * cap, d_model), BF16),
                        pltpu.VMEM((2 * no * cap, d_model), BF16),
                        pltpu.VMEM((2 * no * cap, d_model), BF16),
                        pltpu.VMEM((slots, d_model), BF16),
                        pltpu.VMEM((2 * slots, d_model), BF16),
                        pltpu.VMEM((slots, d_model), BF16),
                        pltpu.VMEM((nc * cap, d_model), BF16),
                        pltpu.VMEM((2 * nc * cap, d_model), BF16),
                        pltpu.VMEM((2 * n_exp, cap), I32),
                        pltpu.VMEM((2 * n_exp, cap), I32),
                        pltpu.VMEM((4 * n_exp, cap), I32),
                        pltpu.VMEM((n_tok, 2 * cap), BF16),
                        pltpu.VMEM((n_tok, d_model), F32),
                        pltpu.VMEM((cap, d_model), F32),
                        pltpu.VMEM((W_SLOTS, d_model, d_ff), BF16),
                        pltpu.VMEM((W_SLOTS, d_ff, d_model), BF16),
                        dma((2, W_SLOTS)),
                        dma, dma((no,)), dma, dma((no,)), dma, dma((n_exp,)), dma, dma((nc,)), dma, dma((nc,)),
                    ],
                    compiler_params=pltpu.CompilerParams(
                        collective_id=1 + i, has_side_effects=True, vmem_limit_bytes=54 * 1024 * 1024),
                )(chip_tok, xown, meta, gate, w_in, w_out)

            return run

        return lax.switch(bucket[0], [branch(i) for i in range(len(sizes))], chip_tok, xown, meta, gate, w_in, w_out)

    return jax.shard_map(local_layer, mesh=mesh, in_specs=(row_spec, row_spec, row_spec, expert_spec, expert_spec),
                         out_specs=row_spec, check_vma=False)
```

profile of v0, /device:TPU:0, one launch (start us, length us, event | category | flops | bytes accessed | tf_op | source)
XLA Modules:
  0.0 62.4 jit_solution(10652602164562077723)
XLA Ops:
  0.0 0.0 copy-start
  0.0 8.4 %shard_map.60 = (bf16[2048,768]{1,0:T(8,128)(2,1)S(1)}, bf16[1024,768]{1,0:T(8,128)(2,1)S(1)}, s32[2,32,128]{2,1,0:T(8,128)S(1)}, s32[1]{0:T(128)}) custom-call(bf16[1024,768]{1,0:T(8,128)(2,1)} %tok.1, s32[8,128]{1,0:T(8,128)} %idx.1), custom_call_target="tpu_custom_call" | custom-call | tf_op jit(solution)/shard_map/pallas_call | solution.py:506
  8.9 0.0 copy-done
  8.9 52.3 %conditional.1 = (bf16[1024,768]{1,0:T(8,128)(2,1)S(1)}) conditional(s32[]{:T(128)} %bitcast, (bf16[2048,768]{1,0:T(8,128)(2,1)S(1)}, bf16[1024,768]{1,0:T(8,128)(2,1)S(1)}, s32[2,32,128]{2,1,0:T(8,128)S(1)}, f32[8,128]{1,0:T(8,128)S(1)}, bf16[8,768,3072]{2,1,0:T(8,128)(2,1)}, ...), branch_computations={%region_0.0_spmd, %region_1.0_spmd, %region_2.0_spmd, %region_3.0_... | conditional | bytes 8 | solution.py:560
  9.1 51.6 %branch_1_fun.1 = bf16[1024,768]{1,0:T(8,128)(2,1)S(1)} custom-call(bf16[2048,768]{1,0:T(8,128)(2,1)S(1)} %get-tuple-element.77.chip_tok, bf16[1024,768]{1,0:T(8,128)(2,1)S(1)} %get-tuple-element.78.xown, s32[2,32,128]{2,1,0:T(8,128)S(1)} %get-tuple-element.79.meta_v, f32[8,128]{1,0:T(8,128)S(1)} %get-tuple-element.80.gate_v, ...), custom_call_target="tpu_custom_call" | custom-call | tf_op jit(solution)/shard_map/cond/branch_1_fun/pallas_call | solution.py:529
  61.2 1.1 %copy.17 = bf16[1024,768]{1,0:T(8,128)(2,1)} copy(bf16[1024,768]{1,0:T(8,128)(2,1)S(1)} %get-tuple-element.109) | data formatting | bytes 3145728
Async XLA Ops:
  0.0 8.9 %copy-start = (f32[8,128]{1,0:T(8,128)S(1)}, f32[8,128]{1,0:T(8,128)}, u32[]{:S(2)}) copy-start(f32[8,128]{1,0:T(8,128)} %param.12) | copy-start | bytes 12292
where the time goes:
time: 62.5 us; the launch traced here: 62.4 us
  Pallas kernels  59.9 us (96%)
  local copies, waits for them, and re-layouts  1.15 us (2%)
  loops' own time  0.73 us (1%)
    pallas_call x1, Pallas kernels, run(): pl.pallas_call(functools.partial(layer_kernel, k_out, k_rows), out_shape=...  51.6 us
    pallas_call x1, Pallas kernels, local_layer(): pl.pallas_call(functools.partial(plan_kernel, n_dp, n_ep, sizes), out_sha...  8.36 us

commit v1 on v0

--- a/solution.py
+++ b/solution.py
@@ -480,9 +480,7 @@
     back_wait(last)
     with jax.named_scope("last_add"):
         back = rland[2 * last * cap:2 * nc * cap, :]
-        for b in range(n_blk):
-            r = at(b * blk, blk)
-            out[r, :] = (acc[r, :] + jnp.dot(hot_last[r, :], back, preferred_element_type=F32)).astype(BF16)
+        out[...] = (acc[...] + jnp.dot(hot_last[...], back, preferred_element_type=F32)).astype(BF16)
 
     sent(g_ss, rland, nc)
 

time: 62.5 us -> 62.5 us (level)
  no operation moved by 1% of the time
where the time goes in v1:
time: 62.5 us; the launch traced here: 62.4 us
  Pallas kernels  59.9 us (96%)
  local copies, waits for them, and re-layouts  1.15 us (2%)
  loops' own time  0.73 us (1%)
    pallas_call x1, Pallas kernels, run(): pl.pallas_call(functools.partial(layer_kernel, k_out, k_rows), out_shape=...  51.6 us
    pallas_call x1, Pallas kernels, local_layer(): pl.pallas_call(functools.partial(plan_kernel, n_dp, n_ep, sizes), out_sha...  8.36 us

profile of v1, /device:TPU:0, one launch (start us, length us, event | category | flops | bytes accessed | tf_op | source)
XLA Modules:
  0.0 62.4 jit_solution(7812485092809254532)
XLA Ops:
  0.0 0.0 copy-start
  0.0 8.4 %shard_map.60 = (bf16[2048,768]{1,0:T(8,128)(2,1)S(1)}, bf16[1024,768]{1,0:T(8,128)(2,1)S(1)}, s32[2,32,128]{2,1,0:T(8,128)S(1)}, s32[1]{0:T(128)}) custom-call(bf16[1024,768]{1,0:T(8,128)(2,1)} %tok.1, s32[8,128]{1,0:T(8,128)} %idx.1), custom_call_target="tpu_custom_call" | custom-call | tf_op jit(solution)/shard_map/pallas_call | solution.py:504
  8.9 0.0 copy-done
  8.9 52.3 %conditional.1 = (bf16[1024,768]{1,0:T(8,128)(2,1)S(1)}) conditional(s32[]{:T(128)} %bitcast, (bf16[2048,768]{1,0:T(8,128)(2,1)S(1)}, bf16[1024,768]{1,0:T(8,128)(2,1)S(1)}, s32[2,32,128]{2,1,0:T(8,128)S(1)}, f32[8,128]{1,0:T(8,128)S(1)}, bf16[8,768,3072]{2,1,0:T(8,128)(2,1)}, ...), branch_computations={%region_0.0_spmd, %region_1.0_spmd, %region_2.0_spmd, %region_3.0_... | conditional | bytes 8 | solution.py:558
  9.1 51.6 %branch_1_fun.1 = bf16[1024,768]{1,0:T(8,128)(2,1)S(1)} custom-call(bf16[2048,768]{1,0:T(8,128)(2,1)S(1)} %get-tuple-element.77.chip_tok, bf16[1024,768]{1,0:T(8,128)(2,1)S(1)} %get-tuple-element.78.xown, s32[2,32,128]{2,1,0:T(8,128)S(1)} %get-tuple-element.79.meta_v, f32[8,128]{1,0:T(8,128)S(1)} %get-tuple-element.80.gate_v, ...), custom_call_target="tpu_custom_call" | custom-call | tf_op jit(solution)/shard_map/cond/branch_1_fun/pallas_call | solution.py:527
  61.2 1.1 %copy.17 = bf16[1024,768]{1,0:T(8,128)(2,1)} copy(bf16[1024,768]{1,0:T(8,128)(2,1)S(1)} %get-tuple-element.109) | data formatting | bytes 3145728
Async XLA Ops:
  0.0 8.9 %copy-start = (f32[8,128]{1,0:T(8,128)S(1)}, f32[8,128]{1,0:T(8,128)}, u32[]{:S(2)}) copy-start(f32[8,128]{1,0:T(8,128)} %param.12) | copy-start | bytes 12292
